TPU v7x, 32 devices: a whole 2x2x4 slice. The times are simulated.
32 devices in a mesh: lat: 16 (over z, x, core), tm: 2 (over y).
Axes of the slice: x: 2, y: 2, z: 4, core: 2. Of those that a mesh axis runs over, the one named last changes fastest.
Arguments:
- fields: bfloat16 [512, 64, 1024], P('lat', 'tm'), may hold values from -16 to 16
Outputs:
- covariance: float32 [64, 64], P('tm')
All inputs are finite; a program needn't handle non-finite values.
Results may differ from a plain program's by a relative error of at most 0.0003.
Values may be sent and summed in bfloat16 or wider, within the bound.
No kernel may reach another device: no remote copies, remote signals or barrier semaphores. Data moves between devices by JAX's collectives and lax.ppermute only.
A program may use at most 64 MiB of HBM per device.

v0:
```python
import math

import jax
import jax.numpy as jnp
from jax import lax
from jax.sharding import PartitionSpec as P

TRUNC = 341
MSLOT = 384
DSLOT = 384


def start_value(order, sine_lat):
    log_start = 0.5 * (
        math.log(0.5)
        + lax.lgamma(order + 1.5)
        - (0.5 * math.log(math.pi) - math.log(2.0))
        - lax.lgamma(order + 1.0)
    ) + order * jnp.log(sine_lat)
    taper = jnp.clip((log_start + 70.0) / 10.0, 0.0, 1.0)
    return jnp.exp(jnp.maximum(log_start, -80.0)) * taper


def step_factors(order, degree):
    top = jnp.sqrt((4.0 * degree * degree - 1.0) / (degree * degree - order * order))
    below = degree - 1.0
    back = jnp.sqrt(
        jnp.maximum(below * below - order * order, 0.0) / jnp.abs(4.0 * below * below - 1.0)
    )
    return (top, top * back)


def legendre_blocks(orders, cosine_lat, sine_lat):
    order_total = orders.shape[0]
    lat_total = cosine_lat.shape[0]
    block_total = 16
    block_length = DSLOT // block_total
    order_grid = orders[:, None, None]
    cosine_grid = cosine_lat[None, :, None]
    block_base = (jnp.arange(block_total) * block_length).astype(jnp.float32)[None, None, :]
    unit = jnp.ones((order_total, lat_total, block_total), jnp.float32)
    empty = jnp.zeros_like(unit)

    def compose(position, matrices):
        upper_left, upper_right, lower_left, lower_right = matrices
        top, mixed = step_factors(
            order_grid, order_grid + block_base + position.astype(jnp.float32)
        )
        diagonal_term = top * cosine_grid
        return (
            diagonal_term * upper_left - mixed * lower_left,
            diagonal_term * upper_right - mixed * lower_right,
            upper_left,
            upper_right,
        )

    upper_left, upper_right, lower_left, lower_right = lax.fori_loop(
        1, block_length + 1, compose, (unit, empty, empty, unit)
    )
    current = start_value(orders[:, None], sine_lat[None, :])
    previous = jnp.zeros_like(current)
    current_list = []
    previous_list = []
    for block in range(block_total):
        current_list.append(current)
        previous_list.append(previous)
        current, previous = (
            upper_left[:, :, block] * current + upper_right[:, :, block] * previous,
            lower_left[:, :, block] * current + lower_right[:, :, block] * previous,
        )
    current = jnp.stack(current_list, axis=-1)
    previous = jnp.stack(previous_list, axis=-1)
    outputs = []
    for position in range(1, block_length + 1):
        outputs.append(current)
        top, mixed = step_factors(order_grid, order_grid + block_base + float(position))
        current, previous = (top * cosine_grid * current - mixed * previous, current)
    values = jnp.stack(outputs, axis=-1)
    return values.reshape(order_total, lat_total, DSLOT)


def weighted_basis(orders, cosine_lat, sine_lat, weight):
    values = legendre_blocks(orders, cosine_lat, sine_lat)
    offsets = jnp.arange(DSLOT).astype(jnp.float32)
    keep = (orders[:, None] + offsets[None, :] <= TRUNC).astype(jnp.float32)
    factor = jnp.where(orders > 0, math.sqrt(2.0), 1.0)
    table = values * keep[:, None, :] * weight[None, :, None] * factor[:, None, None]
    return table.astype(jnp.bfloat16)


def local(fields):
    row_count, month_count, lon_count = fields.shape
    lat_devices = lax.axis_size("lat")
    slots_dev = MSLOT // lat_devices
    lat_index = lax.axis_index("lat")
    column = jnp.arange(2 * MSLOT)
    group = column // (2 * slots_dev)
    inner = column % (2 * slots_dev) // 2
    part_index = column % 2
    own_inner = jnp.arange(slots_dev)
    wave_order = group * slots_dev + inner
    own_order = lat_index * slots_dev + own_inner
    longitude = jnp.arange(lon_count)
    phase = (
        2.0
        * math.pi
        * (wave_order[:, None] * longitude[None, :] % lon_count).astype(jnp.float32)
        / lon_count
    )
    active = (wave_order <= TRUNC).astype(jnp.float32)[:, None]
    transform = (
        jnp.where(part_index[:, None] == 0, jnp.cos(phase), -jnp.sin(phase))
        * active
        / math.sqrt(lon_count)
    )
    transform = transform.astype(jnp.bfloat16)
    flat_fields = fields.reshape(row_count * month_count, lon_count)
    fourier = lax.dot_general(
        transform, flat_fields, (((1,), (1,)), ((), ())), preferred_element_type=jnp.float32
    )
    fourier = fourier.astype(jnp.bfloat16).reshape(2 * MSLOT, row_count, month_count)
    moved = lax.all_to_all(fourier, "lat", split_axis=0, concat_axis=1, tiled=True)
    lat_count = moved.shape[1]
    theta = math.pi * (jnp.arange(lat_count).astype(jnp.float32) + 0.5) / lat_count
    cosine_lat = jnp.cos(theta)
    sine_lat = jnp.sin(theta)
    weight = math.pi * sine_lat / lat_count
    basis = weighted_basis(own_order.astype(jnp.float32), cosine_lat, sine_lat, weight)
    moved_data = moved.reshape(slots_dev, 2, lat_count, month_count)
    coefficients = jnp.einsum(
        "srjt,sjd->tsrd", moved_data, basis, preferred_element_type=jnp.float32
    )
    coefficients = coefficients.astype(jnp.bfloat16).reshape(month_count, -1)
    tm_devices = lax.axis_size("tm")
    total_months = month_count * tm_devices
    columns = lax.all_to_all(coefficients, "tm", split_axis=1, concat_axis=0, tiled=True)
    partial_gram = lax.psum_scatter(
        lax.dot_general(
            columns, columns, (((1,), (1,)), ((), ())), preferred_element_type=jnp.float32
        ),
        "tm",
        scatter_dimension=0,
        tiled=True,
    )
    gram = lax.psum(partial_gram, "lat")
    own_block = lax.dynamic_slice_in_dim(gram, lax.axis_index("tm") * month_count, month_count, 1)
    trace_total = lax.psum(jnp.sum(jnp.diagonal(own_block)), "tm")
    return total_months * gram / (trace_total + 1e-06)


def solution(mesh):
    placed = (P("lat", "tm", None),)
    return jax.shard_map(
        local, mesh=mesh, in_specs=placed, out_specs=P("tm", None), check_vma=False
    )
```

profile of v0, /device:TPU:0, one launch (start us, length us, event | category | flops | bytes accessed | tf_op | source)
XLA Modules:
  0.0 353.8 jit_solution(13318265986543368269)
XLA Ops:
  8.1 16.4 %convolution_convert_fusion = bf16[768,1024]{1,0:T(8,128)(2,1)} fusion(bf16[1024,1024]{1,0:T(8,128)(2,1)S(1)} %bitcast.84, f32[768]{0:T(1024)S(1)} %get-tuple-element.432, s32[768]{0:T(1024)S(1)} %fusion.324, pred[768]{0:T(1024)(128)(4,1)S(1)} %get-tuple-element.431), kind=kOutput, calls=%fused_computation.41 | convolution fusion | flops 1626341376 | bytes 3676928 | tf_op jit(solution)/shard_map/dot_general | solution.py:118
  26.2 9.2 %copy.128 = bf16[768,32,32]{2,1,0:T(8,128)(2,1)} copy(bf16[768,32,32]{0,2,1:T(8,128)(2,1)S(1)} %bitcast.90) | data formatting | bytes 3145728 | tf_op jit(solution)/shard_map/reshape | solution.py:121
  35.4 9.3 %reshape.8823 = bf16[16,2,24576]{2,1,0:T(2,128)(2,1)} reshape(bf16[768,32,32]{2,1,0:T(8,128)(2,1)} %copy.128) | data formatting | bytes 3145728
  44.7 7.4 %all-to-all-start = ((bf16[16,2,24576]{2,1,0:T(2,128)(2,1)}), bf16[16,2,24576]{2,1,0:T(2,128)(2,1)}, u32[]{:S(2)}, u32[]{:S(2)}) async-start(bf16[16,2,24576]{2,1,0:T(2,128)(2,1)} %reshape.8823), calls=%async_computation | async-start | bytes 3145728 | tf_op jit(solution)/shard_map/all_to_all | solution.py:122
  53.3 71.6 %while.25 = (s32[]{:T(128)}, f32[24,512,16]{1,2,0:T(8,128)S(1)}, f32[24,512,16]{1,2,0:T(8,128)}, f32[24,512,16]{1,2,0:T(8,128)S(1)}, f32[24,512,16]{1,2,0:T(8,128)S(1)}, /*index=5*/s32[]{:T(128)}, s32[]{:T(128)}, s32[]{:T(128)}) while((s32[]{:T(128)}, f32[24,512,16]{1,2,0:T(8,128)S(1)}, ...), condition=%wide.region_1.2_spmd.clone.clone.clone, body=%wide.region_0.1_spmd.clone.clone.clone.sunk | while | flops 1778076 | bytes 6308475 | solution.py:57
  58.6 2.7 fusion.362
  61.6 2.7 fusion.362
  64.6 2.7 fusion.362
  70.7 2.7 fusion.362
  73.7 2.7 fusion.362
  76.7 2.7 fusion.362
  82.8 2.7 fusion.362
  125.6 6.1 %add_bitcast_fusion = (f32[24,512,1,1]{1,2,3,0:T(1,128)S(1)}, f32[24,512,1]{1,2,0:T(1,128)S(1)}, f32[24,512,1]{1,2,0:T(1,128)S(1)}, f32[24,512,1]{1,2,0:T(1,128)...) fusion(f32[24,512,16]{1,2,0:T(8,128)S(1)} %get-tuple-element.24, ...), kind=kLoop, calls=%fused_computation.123 | loop fusion | flops 1155072 | bytes 4278464 | tf_op jit(solution)/shard_map/stack | solution.py:72
  152.9 3.0 stack.164
  186.8 17.4 %copy.126 = f32[24,512,16,24]{1,3,2,0:T(8,128)S(1)} copy(f32[24,512,16,24]{1,2,3,0:T(8,128)} %subtract_dynamic-update-slice_fusion) | data formatting | bytes 37748736 | tf_op jit(solution)/shard_map/stack | solution.py:78
  204.4 6.3 %fusion.20 = bf16[24,512,384]{1,2,0:T(8,128)(2,1)} fusion(f32[24,512,16,24]{1,3,2,0:T(8,128)S(1)} %copy.126, f32[24]{0:T(128)S(1)} %copy-done.23, f32[512]{0:T(512)S(1)} %fusion.337, f32[24,384]{1,0:T(8,128)S(1)} %fusion.38), kind=kLoop, calls=%fused_computation.30 | loop fusion | flops 18874368 | bytes 28350560 | tf_op jit(solution)/shard_map/convert_element_type | solution.py:88
  210.6 7.9 %reshape.8824 = bf16[768,32,32]{2,1,0:T(8,128)(2,1)} reshape(bf16[16,2,24576]{2,1,0:T(2,128)(2,1)} %all-to-all-done) | data formatting | bytes 3145728
  218.5 9.5 %copy.129 = bf16[16,48,32,32]{2,0,3,1:T(8,128)(2,1)} copy(bf16[16,48,32,32]{3,2,1,0:T(8,128)(2,1)} %bitcast.85) | data formatting | bytes 3145728 | tf_op jit(solution)/shard_map/all_to_all | solution.py:122
  228.0 9.3 %reshape.8814 = bf16[24,2,512,32]{2,3,1,0:T(8,128)(2,1)} reshape(bf16[48,16,32,32]{2,1,3,0:T(8,128)(2,1)} %bitcast.86) | data formatting | bytes 3145728 | tf_op jit(solution)/shard_map/reshape | solution.py:129
  237.3 7.0 %fusion.352 = f32[24,384,64]{1,2,0:S(1)} fusion(bf16[24,512,384]{1,2,0:T(8,128)(2,1)} %fusion.20, bf16[24,512,64]{1,2,0:T(8,128)(2,1)} %bitcast.89), kind=kOutput, calls=%fused_computation.517 | convolution fusion | flops 603979776 | bytes 13369344
  248.6 18.3 %all_to_all.34 = bf16[32,2,9216]{2,0,1:T(8,128)(2,1)S(1)} all-to-all(bf16[32,2,9216]{2,0,1:T(8,128)(2,1)S(1)} %copy.132), channel_id=1, replica_groups=mesh['lat'=16,'tm'=2] {'tm'}, dimensions={1} | all-to-all | bytes 2359296 | tf_op jit(solution)/shard_map/all_to_all | solution.py:136
  267.9 10.2 %reduce-scatter.2.cloned.1.call-done = f32[32,64]{1,0:T(8,128)} async-done(((f32[64,64]{1,0:T(8,128)}), f32[32,64]{1,0:T(8,128)}) %reduce-scatter.2.cloned.1.call-update) | async-done | bytes 8208 | tf_op jit(solution)/shard_map/reduce_scatter | solution.py:137
  278.1 60.6 %psum.14 = f32[32,64]{1,0:T(8,128)S(1)} all-reduce(f32[32,64]{1,0:T(8,128)} %reduce-scatter.2.cloned.1.call-done), channel_id=1, replica_groups=mesh['lat'=16,'tm'=2] {'lat'}, use_global_device_ids=true, to_apply=%region_3.4 | all-reduce | flops 2048 | bytes 16384 | tf_op jit(solution)/shard_map/psum | solution.py:145
  340.1 5.5 %psum.15 = f32[]{:T(128)} all-reduce(f32[]{:T(128)} %reduce_sum.9), channel_id=1, replica_groups=mesh['lat'=16,'tm'=2] {'tm'}, use_global_device_ids=true, to_apply=%region_5.6 | all-reduce | flops 1 | bytes 8 | tf_op jit(solution)/shard_map/psum | solution.py:147
  (338 shorter events, 116.8 us)
Async XLA Ops:
  44.7 165.9 %all-to-all-start = ((bf16[16,2,24576]{2,1,0:T(2,128)(2,1)}), bf16[16,2,24576]{2,1,0:T(2,128)(2,1)}, u32[]{:S(2)}, u32[]{:S(2)}) async-start(bf16[16,2,24576]{2,1,0:T(2,128)(2,1)} %reshape.8823), calls=%async_computation | async-start | bytes 3145728 | tf_op jit(solution)/shard_map/all_to_all | solution.py:122
  52.2 226.0 %reduce-scatter.2.cloned.1.call-start = ((), (), s32[]{:S(2)}) async-start(), calls=%async_computation.3 | async-start | bytes 49152 | tf_op jit(solution)/shard_map/reduce_scatter | solution.py:137
  52.4 82.7 %copy-start.21 = (f32[24]{0:T(128)}, f32[24]{0:T(128)S(1)}, u32[]{:S(2)}) copy-start(f32[24]{0:T(128)S(1)} %add_convert_fusion) | copy-start | bytes 292
  152.8 13.9 %copy-start.13 = (f32[24,16]{1,0:T(8,128)S(1)}, f32[24,16]{1,0:T(8,128)}, u32[]{:S(2)}) copy-start(f32[24,16]{1,0:T(8,128)} %copy.93) | copy-start | bytes 4612
  152.8 17.5 %copy-start.12 = (f32[24,16]{1,0:T(8,128)S(1)}, f32[24,16]{1,0:T(8,128)}, u32[]{:S(2)}) copy-start(f32[24,16]{1,0:T(8,128)} %copy.100) | copy-start | bytes 4612
  152.8 17.5 %copy-start.14 = (f32[24,16]{1,0:T(8,128)S(1)}, f32[24,16]{1,0:T(8,128)}, u32[]{:S(2)}) copy-start(f32[24,16]{1,0:T(8,128)} %copy.99) | copy-start | bytes 4612
  152.8 18.8 %copy-start.9 = (f32[24,16]{1,0:T(8,128)S(1)}, f32[24,16]{1,0:T(8,128)}, u32[]{:S(2)}) copy-start(f32[24,16]{1,0:T(8,128)} %copy.101) | copy-start | bytes 4612
  152.8 18.8 %copy-start.11 = (f32[24,16]{1,0:T(8,128)S(1)}, f32[24,16]{1,0:T(8,128)}, u32[]{:S(2)}) copy-start(f32[24,16]{1,0:T(8,128)} %copy.102) | copy-start | bytes 4612
  157.1 18.2 %copy-start.8 = (f32[24,16]{1,0:T(8,128)S(1)}, f32[24,16]{1,0:T(8,128)}, u32[]{:S(2)}) copy-start(f32[24,16]{1,0:T(8,128)} %copy.107) | copy-start | bytes 4612
  157.1 18.2 %copy-start.10 = (f32[24,16]{1,0:T(8,128)S(1)}, f32[24,16]{1,0:T(8,128)}, u32[]{:S(2)}) copy-start(f32[24,16]{1,0:T(8,128)} %copy.108) | copy-start | bytes 4612
  158.3 18.3 %copy-start.6 = (f32[24,16]{1,0:T(8,128)S(1)}, f32[24,16]{1,0:T(8,128)}, u32[]{:S(2)}) copy-start(f32[24,16]{1,0:T(8,128)} %copy.109) | copy-start | bytes 4612
  158.3 18.3 %copy-start.7 = (f32[24,16]{1,0:T(8,128)S(1)}, f32[24,16]{1,0:T(8,128)}, u32[]{:S(2)}) copy-start(f32[24,16]{1,0:T(8,128)} %copy.110) | copy-start | bytes 4612
  162.3 16.7 %copy-start.4 = (f32[24,16]{1,0:T(8,128)S(1)}, f32[24,16]{1,0:T(8,128)}, u32[]{:S(2)}) copy-start(f32[24,16]{1,0:T(8,128)} %copy.113) | copy-start | bytes 4612
  162.3 16.7 %copy-start.5 = (f32[24,16]{1,0:T(8,128)S(1)}, f32[24,16]{1,0:T(8,128)}, u32[]{:S(2)}) copy-start(f32[24,16]{1,0:T(8,128)} %copy.114) | copy-start | bytes 4612
  164.6 15.6 %copy-start.2 = (f32[24,16]{1,0:T(8,128)S(1)}, f32[24,16]{1,0:T(8,128)}, u32[]{:S(2)}) copy-start(f32[24,16]{1,0:T(8,128)} %copy.115) | copy-start | bytes 4612
  164.6 15.7 %copy-start.3 = (f32[24,16]{1,0:T(8,128)S(1)}, f32[24,16]{1,0:T(8,128)}, u32[]{:S(2)}) copy-start(f32[24,16]{1,0:T(8,128)} %copy.116) | copy-start | bytes 4612
  168.0 14.5 %copy-start.20 = (f32[24,16]{0,1:T(8,128)S(1)}, f32[24,16]{0,1:T(8,128)}, u32[]{:S(2)}) copy-start(f32[24,16]{0,1:T(8,128)} %get-tuple-element.404) | copy-start | bytes 4612
  168.0 14.6 %copy-start.19 = (f32[24,16]{0,1:T(8,128)S(1)}, f32[24,16]{0,1:T(8,128)}, u32[]{:S(2)}) copy-start(f32[24,16]{0,1:T(8,128)} %get-tuple-element.408) | copy-start | bytes 4612
  168.0 14.7 %copy-start.18 = (f32[24,16]{0,1:T(8,128)S(1)}, f32[24,16]{0,1:T(8,128)}, u32[]{:S(2)}) copy-start(f32[24,16]{0,1:T(8,128)} %get-tuple-element.405) | copy-start | bytes 4612
  168.0 14.7 %copy-start.17 = (f32[24,16]{0,1:T(8,128)S(1)}, f32[24,16]{0,1:T(8,128)}, u32[]{:S(2)}) copy-start(f32[24,16]{0,1:T(8,128)} %get-tuple-element.407) | copy-start | bytes 4612
  168.0 14.8 %copy-start.16 = (f32[24,16]{0,1:T(8,128)S(1)}, f32[24,16]{0,1:T(8,128)}, u32[]{:S(2)}) copy-start(f32[24,16]{0,1:T(8,128)} %get-tuple-element.383) | copy-start | bytes 4612
  186.8 17.5 %copy-start.22 = (f32[24]{0:T(128)S(1)}, f32[24]{0:T(128)}, u32[]{:S(2)}) copy-start(f32[24]{0:T(128)} %copy-done.21) | copy-start | bytes 292
  186.8 17.5 %copy-start.23 = (f32[24]{0:T(128)S(1)}, f32[24]{0:T(128)}, u32[]{:S(2)}) copy-start(f32[24]{0:T(128)} %get-tuple-element.429) | copy-start | bytes 292
  218.5 128.4 %copy-start.1 = (bf16[32,32,1024]{2,1,0:T(8,128)(2,1)S(1)}, bf16[32,32,1024]{2,1,0:T(8,128)(2,1)}, u32[]{:S(2)}) copy-start(bf16[32,32,1024]{2,1,0:T(8,128)(2,1)} %param.3) | copy-start | bytes 6291460
  (2 other events, 15.5 us)
Sparse Core Ops, SparseCore 0:
  268.0 10.0 reduce-scatter.1
where the time goes:
time: 356 us; the launch traced here: 354 us
  other arithmetic  115 us (32%)
  local copies, waits for them, and re-layouts  96.8 us (27%)
  blocking collectives  84.4 us (24%)
  matrix products  24.4 us (7%)
  between operations  14.4 us (4%)
  waiting for transfers between devices  10.2 us (3%)
  starting transfers between devices  7.65 us (2%)
    sub x24, other arithmetic, compose(): diagonal_term * upper_right - mixed * lower_right  63.1 us
    psum x1, blocking collectives, local(): gram = lax.psum(partial_gram, 'lat')  60.6 us
    unnamed x24, other arithmetic  29 us
    unnamed x51, local copies, waits for them, and re-layouts  19.8 us
    all_to_all x1, blocking collectives, local(): lax.all_to_all(coefficients, 'tm', split_axis=1, concat_axis=0, tiled=True)  18.3 us
    another operation x1, local copies, waits for them, and re-layouts, legendre_blocks(): values = jnp.stack(outputs, axis=-1)  17.4 us
    dot_general x1, matrix products, local(): lax.dot_general(transform, flat_fields, (((1,), (1,)), ((), ())), preferr...  16.4 us
    reduce_scatter x1, waiting for transfers between devices, local(): lax.psum_scatter(lax.dot_general(columns, columns, (((1,), (1,)), ((), ()...  10.2 us
  transfers between devices with their start and end apart: 2, of which 1 were waited for; matrix products, arithmetic and copies ran while one was open for 45% of the time, Pallas kernels for 0%

commit v1 on v0

v1 whole, which is shorter than its diff:
```python
import math

import numpy as np
import jax
import jax.numpy as jnp
from jax import lax
from jax.experimental import pallas as pl
from jax.experimental.pallas import tpu as pltpu
from jax.sharding import PartitionSpec as P

TRUNC = 341
LANES = 128
SUB = 8
STEPS = 32
SCALE = 2.0**16


def transform_table(lon_count, device_total, slot_total):
    order = np.arange(slot_total)[None, :] * device_total + np.arange(device_total)[:, None]
    order = order.reshape(-1, 1)
    phase = 2.0 * np.pi * (order * np.arange(lon_count)[None, :] % lon_count) / lon_count
    active = (order <= TRUNC) / np.sqrt(lon_count)
    table = np.stack([np.cos(phase) * active, -np.sin(phase) * active], axis=1)
    return table.reshape(-1, lon_count).astype(np.float32).astype(jnp.bfloat16)


def transform_kernel(table_ref, fields_ref, out_ref, scratch_ref):
    step = pl.program_id(0)
    groups = out_ref.shape[1]
    column_total, lon_count = table_ref.shape
    block = fields_ref[...].reshape(-1, lon_count)
    values = lax.dot_general(
        table_ref[...], block, (((1,), (1,)), ((), ())), preferred_element_type=jnp.float32
    )
    for part in range(values.shape[1] // LANES):
        group = step * (values.shape[1] // LANES) + part
        scratch_ref[pl.ds(group, column_total, stride=groups), :] = values[
            :, part * LANES : (part + 1) * LANES
        ]

    @pl.when(step == pl.num_programs(0) - 1)
    def _():
        out_ref[...] = scratch_ref[...].reshape(out_ref.shape).astype(out_ref.dtype)


def longitude_transform(fields, table, groups):
    row_count, month_count, lon_count = fields.shape
    column_total = table.shape[0]
    rows_step = 2 * LANES // month_count
    return pl.pallas_call(
        transform_kernel,
        grid=(row_count // rows_step,),
        in_specs=[
            pl.BlockSpec((column_total, lon_count), lambda g: (0, 0)),
            pl.BlockSpec((rows_step, month_count, lon_count), lambda g: (g, 0, 0)),
        ],
        out_specs=pl.BlockSpec((column_total, groups, LANES), lambda g: (0, 0, 0)),
        out_shape=jax.ShapeDtypeStruct((column_total, groups, LANES), jnp.bfloat16),
        scratch_shapes=[pltpu.VMEM((column_total * groups, LANES), jnp.float32)],
        name="transform",
    )(table, fields)


def basis_kernel(order_ref, cosine_ref, start_ref, out_ref, scratch_ref, *, depths, offsets):
    cosine = jnp.broadcast_to(cosine_ref[...], (SUB, cosine_ref.shape[1]))
    for base in range(0, len(depths), SUB):
        order = order_ref[base : base + SUB, :]
        lane = lax.broadcasted_iota(jnp.int32, order.shape, 1).astype(jnp.float32)
        first = start_ref[base : base + SUB, :]
        columns = scratch_ref.shape[0]
        for column in range(columns):
            scratch_ref[column, 0:SUB, :] = first[:, column * LANES : (column + 1) * LANES]

        def block(index, carry, order=order, lane=lane, columns=columns):
            current, previous = carry
            degree = order + (lane + 1.0) + (index * STEPS).astype(jnp.float32)
            top = jnp.sqrt((4.0 * degree * degree - 1.0) / (degree * degree - order * order))
            below = degree - 1.0
            back = jnp.sqrt(
                jnp.maximum(below * below - order * order, 0.0)
                / jnp.abs(4.0 * below * below - 1.0)
            )
            inside = degree <= TRUNC
            mixed = jnp.where(inside, top * back, 0.0)
            top = jnp.where(inside, top, 0.0)
            for step in range(STEPS):
                top_step = top[:, step : step + 1] * cosine
                following = top_step * current - mixed[:, step : step + 1] * previous
                row = pl.multiple_of((index * STEPS + (step + 1)) * SUB, SUB)
                for column in range(columns):
                    scratch_ref[column, pl.ds(row, SUB), :] = following[
                        :, column * LANES : (column + 1) * LANES
                    ]
                current, previous = following, current
            return current, previous

        depth_most = depths[base]
        lax.fori_loop(0, pl.cdiv(depth_most - 1, STEPS), block, (first, jnp.zeros_like(first)))
        for slot in range(base, min(base + SUB, len(depths))):
            depth = depths[slot]
            for column in range(columns):
                rows = scratch_ref[column, pl.ds(slot - base, depth, stride=SUB), :]
                out_ref[
                    offsets[slot] : offsets[slot] + depth, column * LANES : (column + 1) * LANES
                ] = rows.astype(out_ref.dtype)


def basis_blocks(order, cosine, start, depths, offsets):
    lat_total = cosine.shape[1]
    steps_most = pl.cdiv(max(depths) - 1, STEPS) * STEPS + 1
    return pl.pallas_call(
        lambda *refs: basis_kernel(*refs, depths=depths, offsets=offsets),
        out_shape=jax.ShapeDtypeStruct((sum(depths), lat_total), jnp.bfloat16),
        scratch_shapes=[pltpu.VMEM((lat_total // LANES, steps_most * SUB, LANES), jnp.float32)],
        name="basis",
    )(order, cosine, start)


def exchange_blocks(pieces):
    count = len(pieces)
    width = LANES // count
    block = lax.broadcasted_iota(jnp.int32, pieces[0].shape, 1) // width
    distance = count // 2
    while distance >= 1:
        low = (block // distance) % 2 == 0
        shift = distance * width
        following = list(pieces)
        for index in range(count):
            if (index // distance) % 2 == 0:
                first, second = pieces[index], pieces[index + distance]
                following[index] = jnp.where(low, first, pltpu.roll(second, shift, 1))
                following[index + distance] = jnp.where(
                    low, pltpu.roll(first, LANES - shift, 1), second
                )
        pieces = following
        distance //= 2
    return pieces


def gram_kernel(moved_ref, basis_ref, out_ref, *, depths, offsets, row_low):
    lat_devices, tm_devices, _, _, groups, _ = moved_ref.shape
    total = None
    for slot, depth in enumerate(depths):
        pieces = [
            moved_ref[:, tm, slot, part].astype(jnp.float32).reshape(lat_devices * groups, LANES)
            for part in range(2)
            for tm in range(tm_devices)
        ]
        tiles = []
        for begin in range(0, len(pieces), row_low):
            tiles.append(exchange_blocks(pieces[begin : begin + row_low]))
        fourier = jnp.concatenate(
            [
                jnp.concatenate([tile[row] for tile in tiles], axis=1)
                for row in range(row_low)
            ],
            axis=0,
        ).astype(jnp.bfloat16)
        basis = basis_ref[offsets[slot] : offsets[slot] + depth, :]
        coefficients = jnp.dot(basis, fourier, preferred_element_type=jnp.float32)
        coefficients = coefficients.astype(jnp.bfloat16)
        gram = lax.dot_general(
            coefficients,
            coefficients,
            (((0,), (0,)), ((), ())),
            preferred_element_type=jnp.float32,
        )
        total = gram if total is None else total + gram
    months = total.shape[0] // 2
    total = total * (1.0 / (SCALE * SCALE))
    if months * 2 == LANES:
        half = months // 2
        lane = lax.broadcasted_iota(jnp.int32, (half, LANES), 1)
        low = total[0:half] + pltpu.roll(total[months : months + half], months, 1)
        high = pltpu.roll(total[half:months], months, 1) + total[months + half :]
        out_ref[...] = jnp.where(lane < months, low, high)
    else:
        out_ref[...] = total[:months, :months] + total[months:, months:]


def gram_terms(moved, basis, depths, offsets, row_low):
    months = moved.shape[1] * (LANES // row_low)
    shape = (months // 2, LANES) if 2 * months == LANES else (months, months)
    return pl.pallas_call(
        lambda *refs: gram_kernel(*refs, depths=depths, offsets=offsets, row_low=row_low),
        out_shape=jax.ShapeDtypeStruct(shape, jnp.float32),
        name="gram",
    )(moved, basis)


def finish_kernel(parts_ref, out_ref):
    month_total = out_ref.shape[1]
    half = month_total // 2
    total = jnp.sum(parts_ref[...], axis=0)
    row = lax.broadcasted_iota(jnp.int32, total.shape, 0)
    lane = lax.broadcasted_iota(jnp.int32, total.shape, 1)
    diagonal = (lane == row) | (lane == row + (month_total + half))
    trace = jnp.sum(jnp.where(diagonal, total, 0.0))
    total = month_total * total / (trace + 1e-06)
    upper = lax.axis_index("tm") * jnp.ones_like(lane) == 1
    total = jnp.where(upper, pltpu.roll(total, month_total, 1), total)
    out_ref[...] = total[:, :month_total]


def local(fields):
    row_count, month_count, lon_count = fields.shape
    lat_devices = lax.axis_size("lat")
    tm_devices = lax.axis_size("tm")
    device_total = lat_devices * tm_devices
    device = lax.axis_index("lat") * tm_devices + lax.axis_index("tm")
    lat_count = row_count * lat_devices
    months = month_count * tm_devices
    slots = -(-(TRUNC + 1) // device_total)
    row_low = LANES // month_count
    groups = row_count // row_low
    depths = [-(-(TRUNC + 1 - slot * device_total) // 16) * 16 for slot in range(slots)]
    offsets = [sum(depths[:slot]) for slot in range(slots)]

    table = jnp.asarray(transform_table(lon_count, device_total, slots))
    fourier = longitude_transform(fields, table, groups)
    fourier = fourier.reshape(device_total, slots * 2, groups, LANES)
    moved = lax.all_to_all(fourier, ("lat", "tm"), split_axis=0, concat_axis=0, tiled=True)
    moved = moved.reshape(lat_devices, tm_devices, slots, 2, groups, LANES)

    latitude = np.arange(lat_count).reshape(lat_devices, groups, row_low)
    latitude = jnp.asarray(latitude.transpose(2, 0, 1).reshape(1, -1))
    theta = math.pi * (latitude.astype(jnp.float32) + 0.5) / lat_count
    cosine_lat = jnp.cos(theta)
    sine_lat = jnp.sin(theta)
    weight = math.pi * sine_lat / lat_count
    padded = -(-slots // SUB) * SUB
    order = (jnp.arange(padded) * device_total + device).astype(jnp.float32)[:, None]
    log_start = 0.5 * (
        math.log(0.5)
        + lax.lgamma(order + 1.5)
        - (0.5 * math.log(math.pi) - math.log(2.0))
        - lax.lgamma(order + 1.0)
    ) + order * jnp.log(sine_lat)
    taper = jnp.clip((log_start + 70.0) / 10.0, 0.0, 1.0)
    factor = jnp.where(order > 0, math.sqrt(2.0), 1.0) * (order <= TRUNC) * SCALE
    start = jnp.exp(jnp.maximum(log_start, -80.0)) * taper * weight * factor
    basis = basis_blocks(
        jnp.broadcast_to(order, (padded, LANES)), cosine_lat, start, depths, offsets
    )

    gram = gram_terms(moved, basis, depths, offsets, row_low)
    if 2 * months == LANES and tm_devices == 2:
        parts = lax.all_gather(gram, ("lat", "tm"), axis=0, tiled=False)
        return pl.pallas_call(
            finish_kernel,
            out_shape=jax.ShapeDtypeStruct((month_count, months), jnp.float32),
            name="finish",
        )(parts)
    gram = lax.psum(gram, ("lat", "tm")).reshape(-1)
    if 2 * months == LANES:
        gram = gram.reshape(months // 2, 2, months).transpose(1, 0, 2)
    gram = gram.reshape(months, months)
    trace = jnp.sum(jnp.diagonal(gram))
    own = lax.dynamic_slice_in_dim(gram, lax.axis_index("tm") * month_count, month_count, 0)
    return months * own / (trace + 1e-06)


def solution(mesh):
    placed = (P("lat", "tm", None),)
    return jax.shard_map(
        local, mesh=mesh, in_specs=placed, out_specs=P("tm", None), check_vma=False
    )
```

time: 356 us -> 131 us (0.37)
  other arithmetic: 115 us -> 0.77 us
  local copies, waits for them, and re-layouts: 96.8 us -> 1.78 us
  matrix products: 24.4 us -> 0 us
  Pallas kernels: 0 us -> 19 us
  waiting for transfers between devices: 10.2 us -> 27.2 us
  between operations: 14.4 us -> 0.05 us
  blocking collectives: 84.4 us -> 74.3 us
    all_gather x0 -> x1, blocking collectives: none -> 74.3 us  [local(): parts = lax.all_gather(gram, ('lat', 'tm'), axis=0, tiled=False)]
    psum x2 -> x0, blocking collectives: 66.2 us -> none  [the longest x1 60.6 us: local(): gram = lax.psum(partial_gram, 'lat')]
    sub x48 -> x0, other arithmetic: 63.3 us -> none  [the longest x24 63.1 us: compose(): diagonal_term * upper_right - mixed * lower_right]
    unnamed x24 -> x0, other arithmetic: 29 us -> none
    all_to_all x1, waiting for transfers between devices: 0.01 us -> 27.2 us  [local(): lax.all_to_all(fourier, ('lat', 'tm'), split_axis=0, concat_axis=0, tiled...]
    another operation x5 -> x0, local copies, waits for them, and re-layouts: 23.7 us -> none  [the longest x1 17.4 us: legendre_blocks(): values = jnp.stack(outputs, axis=-1)]
    pallas_call x0 -> x4, Pallas kernels: none -> 19 us  [the longest x1 5.94 us: basis_blocks(): pl.pallas_call(lambda *refs: basis_kernel(*refs, depths=depths, offsets=o...]
    unnamed x51 -> x6, local copies, waits for them, and re-layouts: 19.8 us -> 1.11 us
  transfers between devices with their start and end apart: 2 -> 1, of which waited for: 1 -> 1; matrix products, arithmetic and copies ran while one was open for 45% -> 1% of each run, Pallas kernels for 0% -> 5%
where the time goes in v1:
time: 131 us; the launch traced here: 130 us
  blocking collectives  74.3 us (57%)
  waiting for transfers between devices  27.2 us (21%)
  Pallas kernels  19 us (15%)
  starting transfers between devices  7.31 us (6%)
  local copies, waits for them, and re-layouts  1.78 us (1%)
    all_gather x1, blocking collectives, local(): parts = lax.all_gather(gram, ('lat', 'tm'), axis=0, tiled=False)  74.3 us
    all_to_all x1, waiting for transfers between devices, local(): lax.all_to_all(fourier, ('lat', 'tm'), split_axis=0, concat_axis=0, tiled...  27.2 us
    all_to_all x1, starting transfers between devices, local(): lax.all_to_all(fourier, ('lat', 'tm'), split_axis=0, concat_axis=0, tiled...  7.31 us
    pallas_call x1, Pallas kernels, basis_blocks(): pl.pallas_call(lambda *refs: basis_kernel(*refs, depths=depths, offsets=o...  5.94 us
    pallas_call x1, Pallas kernels, longitude_transform(): pl.pallas_call(transform_kernel, grid=(row_count // rows_step,), in_specs...  5.63 us
    pallas_call x1, Pallas kernels, gram_terms(): pl.pallas_call(lambda *refs: gram_kernel(*refs, depths=depths, offsets=of...  5.52 us
  transfers between devices with their start and end apart: 1, of which 1 were waited for; matrix products, arithmetic and copies ran while one was open for 1% of the time, Pallas kernels for 5%

profile of v1, /device:TPU:0, one launch (start us, length us, event | category | flops | bytes accessed | tf_op | source)
XLA Modules:
  0.0 130.4 jit_solution(12021924918279309967)
XLA Ops:
  0.0 5.6 %transform.1 = bf16[704,8,128]{2,1,0:T(8,128)(2,1)} custom-call(bf16[704,1024]{1,0:T(8,128)(2,1)} %constant.102.clone.table_ref, bf16[32,32,1024]{2,1,0:T(8,128)(2,1)} %fields_ref.1), custom_call_target="tpu_custom_call" | custom-call | tf_op jit(solution)/shard_map/transform/pallas_call | solution.py:50
  5.6 0.0 copy-start.1
  5.6 0.0 copy-start.2
  5.6 7.3 %all-to-all-start = ((bf16[32,22,8,128]{3,2,1,0:T(8,128)(2,1)}), bf16[32,22,8,128]{3,2,1,0:T(8,128)(2,1)S(1)}, u32[]{:S(2)}, u32[]{:S(2)}) async-start(bf16[32,22,8,128]{3,2,1,0:T(8,128)(2,1)} %bitcast.4), calls=%async_computation | async-start | bytes 2883584 | tf_op jit(solution)/shard_map/all_to_all | solution.py:222
  13.0 0.1 fusion
  13.0 0.0 copy-done.1
  13.1 0.0 copy-done.2
  13.1 0.7 multiply_multiply_fusion.refs_2_
  13.8 0.7 broadcast_in_dim.12.refs_0_
  14.4 5.9 %basis.1.refs_1_ = bf16[2112,512]{1,0:T(8,128)(2,1)} custom-call(f32[16,128]{1,0:T(8,128)} %broadcast_in_dim.12.refs_0_, f32[1,512]{1,0:T(1,128)} %constant.107.refs_1_, f32[16,512]{1,0:T(8,128)} %multiply_multiply_fusion.refs_2_), custom_call_target="tpu_custom_call" | custom-call | tf_op jit(solution)/shard_map/basis/pallas_call | solution.py:111
  20.4 27.2 %all-to-all-done = bf16[32,22,8,128]{3,2,1,0:T(8,128)(2,1)S(1)} async-done(((bf16[32,22,8,128]{3,2,1,0:T(8,128)(2,1)}), bf16[32,22,8,128]{3,2,1,0:T(8,128)(2,1)S(1)}, u32[]{:S(2)}, u32[]{:S(2)}) %all-to-all-start) | async-done | bytes 1441824 | tf_op jit(solution)/shard_map/all_to_all | solution.py:222
  47.6 0.0 copy-start
  47.6 1.1 copy-done
  48.7 5.5 %gram.1 = f32[32,128]{1,0:T(8,128)} custom-call(bf16[16,2,11,2,8,128]{5,4,3,2,1,0:T(8,128)(2,1)} %bitcast.3, bf16[2112,512]{1,0:T(8,128)(2,1)} %basis.1.refs_1_), custom_call_target="tpu_custom_call" | custom-call | tf_op jit(solution)/shard_map/gram/pallas_call | solution.py:184
  54.2 74.3 %all-gather = f32[1024,128]{1,0:T(8,128)} all-gather(f32[32,128]{1,0:T(8,128)} %gram.1), channel_id=2, replica_groups=mesh['lat'=16,'tm'=2] {'lat','tm'}, dimensions={0}, use_global_device_ids=true | all-gather | bytes 540672 | tf_op jit(solution)/shard_map/all_gather | solution.py:248
  128.5 1.9 %finish.1 = f32[32,64]{1,0:T(8,128)} custom-call(f32[32,32,128]{2,1,0:T(8,128)} %bitcast.5), custom_call_target="tpu_custom_call" | custom-call | tf_op jit(solution)/shard_map/finish/pallas_call | solution.py:249
  (1 shorter events, 0.0 us)
Async XLA Ops:
  5.6 7.4 %copy-start.1 = (f32[512]{0:T(512)S(1)}, f32[512]{0:T(512)}, u32[]{:S(2)}) copy-start(f32[512]{0:T(512)} %constant.112) | copy-start | bytes 6148
  5.6 7.4 %copy-start.2 = (f32[512]{0:T(512)S(1)}, f32[512]{0:T(512)}, u32[]{:S(2)}) copy-start(f32[512]{0:T(512)} %constant.110) | copy-start | bytes 6148
  5.6 42.0 %all-to-all-start = ((bf16[32,22,8,128]{3,2,1,0:T(8,128)(2,1)}), bf16[32,22,8,128]{3,2,1,0:T(8,128)(2,1)S(1)}, u32[]{:S(2)}, u32[]{:S(2)}) async-start(bf16[32,22,8,128]{3,2,1,0:T(8,128)(2,1)} %bitcast.4), calls=%async_computation | async-start | bytes 2883584 | tf_op jit(solution)/shard_map/all_to_all | solution.py:222
  47.6 1.1 copy-start

commit v2 on v1

--- a/solution.py
+++ b/solution.py
@@ -168,19 +168,33 @@
         total = gram if total is None else total + gram
     months = total.shape[0] // 2
     total = total * (1.0 / (SCALE * SCALE))
-    if months * 2 == LANES:
-        half = months // 2
-        lane = lax.broadcasted_iota(jnp.int32, (half, LANES), 1)
-        low = total[0:half] + pltpu.roll(total[months : months + half], months, 1)
-        high = pltpu.roll(total[half:months], months, 1) + total[months + half :]
-        out_ref[...] = jnp.where(lane < months, low, high)
-    else:
+    if len(out_ref.shape) == 2:
         out_ref[...] = total[:months, :months] + total[months:, months:]
-
-
-def gram_terms(moved, basis, depths, offsets, row_low):
+        return
+    half = months // 2
+    quarter = half // 2
+    lane = lax.broadcasted_iota(jnp.int32, (half, LANES), 1)
+    row = lax.broadcasted_iota(jnp.int32, (half, LANES), 0)
+    low = total[0:half] + pltpu.roll(total[months : months + half], months, 1)
+    high = pltpu.roll(total[half:months], months, 1) + total[months + half :]
+    packed = jnp.where(lane < months, low, high)
+    trace = jnp.sum(jnp.where((lane == row) | (lane == row + months + half), packed, 0.0))
+    lane = lane[:quarter]
+    row = row[:quarter]
+    swapped = pltpu.roll(packed, months, 1)
+    halves = (
+        jnp.where(lane < months, packed[:quarter], swapped[quarter:]),
+        jnp.where(lane < months, swapped[:quarter], packed[quarter:]),
+    )
+    for index, value in enumerate(halves):
+        value = jnp.where((row == 1) & (lane == index * half), trace, value)
+        for device in range(index, out_ref.shape[0], 2):
+            out_ref[device] = value
+
+
+def gram_terms(moved, basis, depths, offsets, row_low, spread):
     months = moved.shape[1] * (LANES // row_low)
-    shape = (months // 2, LANES) if 2 * months == LANES else (months, months)
+    shape = (spread, months // 4, LANES) if spread else (months, months)
     return pl.pallas_call(
         lambda *refs: gram_kernel(*refs, depths=depths, offsets=offsets, row_low=row_low),
         out_shape=jax.ShapeDtypeStruct(shape, jnp.float32),
@@ -189,17 +203,18 @@
 
 
 def finish_kernel(parts_ref, out_ref):
-    month_total = out_ref.shape[1]
-    half = month_total // 2
+    half, month_total = out_ref.shape
     total = jnp.sum(parts_ref[...], axis=0)
     row = lax.broadcasted_iota(jnp.int32, total.shape, 0)
     lane = lax.broadcasted_iota(jnp.int32, total.shape, 1)
-    diagonal = (lane == row) | (lane == row + (month_total + half))
-    trace = jnp.sum(jnp.where(diagonal, total, 0.0))
+    corner = lane - lax.axis_index("tm") * half
+    slot = (row == 1) & (corner == 0)
+    trace = jnp.sum(jnp.where(slot, total, 0.0))
+    mirror = jnp.sum(jnp.where((row == 0) & (corner == 1), total, 0.0))
+    total = jnp.where(slot, mirror, total)
     total = month_total * total / (trace + 1e-06)
-    upper = lax.axis_index("tm") * jnp.ones_like(lane) == 1
-    total = jnp.where(upper, pltpu.roll(total, month_total, 1), total)
-    out_ref[...] = total[:, :month_total]
+    out_ref[: half // 2] = total[:, :month_total]
+    out_ref[half // 2 :] = pltpu.roll(total, month_total, 1)[:, :month_total]
 
 
 def local(fields):
@@ -243,18 +258,16 @@
         jnp.broadcast_to(order, (padded, LANES)), cosine_lat, start, depths, offsets
     )
 
-    gram = gram_terms(moved, basis, depths, offsets, row_low)
-    if 2 * months == LANES and tm_devices == 2:
-        parts = lax.all_gather(gram, ("lat", "tm"), axis=0, tiled=False)
+    spread = device_total if 2 * months == LANES and tm_devices == 2 else 0
+    gram = gram_terms(moved, basis, depths, offsets, row_low, spread)
+    if spread:
+        parts = lax.all_to_all(gram, ("lat", "tm"), split_axis=0, concat_axis=0, tiled=True)
         return pl.pallas_call(
             finish_kernel,
             out_shape=jax.ShapeDtypeStruct((month_count, months), jnp.float32),
             name="finish",
         )(parts)
-    gram = lax.psum(gram, ("lat", "tm")).reshape(-1)
-    if 2 * months == LANES:
-        gram = gram.reshape(months // 2, 2, months).transpose(1, 0, 2)
-    gram = gram.reshape(months, months)
+    gram = lax.psum(gram, ("lat", "tm"))
     trace = jnp.sum(jnp.diagonal(gram))
     own = lax.dynamic_slice_in_dim(gram, lax.axis_index("tm") * month_count, month_count, 0)
     return months * own / (trace + 1e-06)

time: 131 us -> 71 us (0.54)
  blocking collectives: 74.3 us -> 14.4 us
    all_gather x1 -> x0, blocking collectives: 74.3 us -> none  [local(): parts = lax.all_gather(gram, ('lat', 'tm'), axis=0, tiled=False)]
    all_to_all x0 -> x1, blocking collectives: none -> 14.4 us  [local(): lax.all_to_all(gram, ('lat', 'tm'), split_axis=0, concat_axis=0, tiled=True)]
  transfers between devices with their start and end apart: 1 -> 1, of which waited for: 1 -> 1; matrix products, arithmetic and copies ran while one was open for 1% -> 2% of each run, Pallas kernels for 5% -> 8%
where the time goes in v2:
time: 71 us; the launch traced here: 70.6 us
  waiting for transfers between devices  27.2 us (38%)
  Pallas kernels  19.1 us (27%)
  blocking collectives  14.4 us (20%)
  starting transfers between devices  7.31 us (10%)
  local copies, waits for them, and re-layouts  1.78 us (3%)
  other arithmetic  0.77 us (1%)
    all_to_all x1, waiting for transfers between devices, local(): lax.all_to_all(fourier, ('lat', 'tm'), split_axis=0, concat_axis=0, tiled...  27.2 us
    all_to_all x1, blocking collectives, local(): lax.all_to_all(gram, ('lat', 'tm'), split_axis=0, concat_axis=0, tiled=True)  14.4 us
    all_to_all x1, starting transfers between devices, local(): lax.all_to_all(fourier, ('lat', 'tm'), split_axis=0, concat_axis=0, tiled...  7.31 us
    pallas_call x1, Pallas kernels, basis_blocks(): pl.pallas_call(lambda *refs: basis_kernel(*refs, depths=depths, offsets=o...  5.94 us
    pallas_call x1, Pallas kernels, gram_terms(): pl.pallas_call(lambda *refs: gram_kernel(*refs, depths=depths, offsets=of...  5.74 us
    pallas_call x1, Pallas kernels, longitude_transform(): pl.pallas_call(transform_kernel, grid=(row_count // rows_step,), in_specs...  5.63 us
    pallas_call x1, Pallas kernels, local(): pl.pallas_call(finish_kernel, out_shape=jax.ShapeDtypeStruct((month_count...  1.78 us
  transfers between devices with their start and end apart: 1, of which 1 were waited for; matrix products, arithmetic and copies ran while one was open for 2% of the time, Pallas kernels for 8%

profile of v2, /device:TPU:0, one launch (start us, length us, event | category | flops | bytes accessed | tf_op | source)
XLA Modules:
  0.0 70.6 jit_solution(2523130042623896174)
XLA Ops:
  0.0 5.6 %transform.1 = bf16[704,8,128]{2,1,0:T(8,128)(2,1)} custom-call(bf16[704,1024]{1,0:T(8,128)(2,1)} %constant.102.clone.table_ref, bf16[32,32,1024]{2,1,0:T(8,128)(2,1)} %fields_ref.1), custom_call_target="tpu_custom_call" | custom-call | tf_op jit(solution)/shard_map/transform/pallas_call | solution.py:50
  5.6 0.0 copy-start.1
  5.6 0.0 copy-start.2
  5.6 7.3 %all-to-all-start = ((bf16[32,22,8,128]{3,2,1,0:T(8,128)(2,1)}), bf16[32,22,8,128]{3,2,1,0:T(8,128)(2,1)S(1)}, u32[]{:S(2)}, u32[]{:S(2)}) async-start(bf16[32,22,8,128]{3,2,1,0:T(8,128)(2,1)} %bitcast.3), calls=%async_computation | async-start | bytes 2883584 | tf_op jit(solution)/shard_map/all_to_all | solution.py:237
  13.0 0.1 fusion
  13.0 0.0 copy-done.1
  13.1 0.0 copy-done.2
  13.1 0.7 multiply_multiply_fusion.refs_2_
  13.8 0.7 broadcast_in_dim.12.refs_0_
  14.4 5.9 %basis.1.refs_1_ = bf16[2112,512]{1,0:T(8,128)(2,1)} custom-call(f32[16,128]{1,0:T(8,128)} %broadcast_in_dim.12.refs_0_, f32[1,512]{1,0:T(1,128)} %constant.107.refs_1_, f32[16,512]{1,0:T(8,128)} %multiply_multiply_fusion.refs_2_), custom_call_target="tpu_custom_call" | custom-call | tf_op jit(solution)/shard_map/basis/pallas_call | solution.py:111
  20.4 27.2 %all-to-all-done = bf16[32,22,8,128]{3,2,1,0:T(8,128)(2,1)S(1)} async-done(((bf16[32,22,8,128]{3,2,1,0:T(8,128)(2,1)}), bf16[32,22,8,128]{3,2,1,0:T(8,128)(2,1)S(1)}, u32[]{:S(2)}, u32[]{:S(2)}) %all-to-all-start) | async-done | bytes 1441824 | tf_op jit(solution)/shard_map/all_to_all | solution.py:237
  47.6 0.0 copy-start
  47.6 1.1 %copy-done = bf16[32,22,8,128]{3,2,1,0:T(8,128)(2,1)} copy-done((bf16[32,22,8,128]{3,2,1,0:T(8,128)(2,1)}, bf16[32,22,8,128]{3,2,1,0:T(8,128)(2,1)S(1)}, u32[]{:S(2)}) %copy-start) | copy-done | bytes 1441816
  48.7 5.7 %gram.1 = f32[32,16,128]{2,1,0:T(8,128)} custom-call(bf16[16,2,11,2,8,128]{5,4,3,2,1,0:T(8,128)(2,1)} %bitcast.2, bf16[2112,512]{1,0:T(8,128)(2,1)} %basis.1.refs_1_), custom_call_target="tpu_custom_call" | custom-call | tf_op jit(solution)/shard_map/gram/pallas_call | solution.py:198
  54.4 14.4 %all_to_all.10.parts_ref = f32[32,16,128]{2,1,0:T(8,128)} all-to-all(f32[32,16,128]{2,1,0:T(8,128)} %gram.1), channel_id=1, replica_groups=mesh['lat'=16,'tm'=2] {'lat','tm'}, dimensions={0} | all-to-all | bytes 524288 | tf_op jit(solution)/shard_map/all_to_all | solution.py:264
  68.8 1.8 %finish.1 = f32[32,64]{1,0:T(8,128)} custom-call(f32[32,16,128]{2,1,0:T(8,128)} %all_to_all.10.parts_ref), custom_call_target="tpu_custom_call" | custom-call | tf_op jit(solution)/shard_map/finish/pallas_call | solution.py:265
  (1 shorter events, 0.0 us)
Async XLA Ops:
  5.6 7.4 %copy-start.1 = (f32[512]{0:T(512)S(1)}, f32[512]{0:T(512)}, u32[]{:S(2)}) copy-start(f32[512]{0:T(512)} %constant.112) | copy-start | bytes 6148
  5.6 7.4 %copy-start.2 = (f32[512]{0:T(512)S(1)}, f32[512]{0:T(512)}, u32[]{:S(2)}) copy-start(f32[512]{0:T(512)} %constant.110) | copy-start | bytes 6148
  5.6 42.0 %all-to-all-start = ((bf16[32,22,8,128]{3,2,1,0:T(8,128)(2,1)}), bf16[32,22,8,128]{3,2,1,0:T(8,128)(2,1)S(1)}, u32[]{:S(2)}, u32[]{:S(2)}) async-start(bf16[32,22,8,128]{3,2,1,0:T(8,128)(2,1)} %bitcast.3), calls=%async_computation | async-start | bytes 2883584 | tf_op jit(solution)/shard_map/all_to_all | solution.py:237
  47.6 1.1 %copy-start = (bf16[32,22,8,128]{3,2,1,0:T(8,128)(2,1)}, bf16[32,22,8,128]{3,2,1,0:T(8,128)(2,1)S(1)}, u32[]{:S(2)}) copy-start(bf16[32,22,8,128]{3,2,1,0:T(8,128)(2,1)S(1)} %all-to-all-done) | copy-start | bytes 4325380

commit v3 on v2

--- a/solution.py
+++ b/solution.py
@@ -13,6 +13,7 @@
 SUB = 8
 STEPS = 32
 SCALE = 2.0**16
+PARAMS = pltpu.CompilerParams(vmem_limit_bytes=32 * 2**20)
 
 
 def transform_table(lon_count, device_total, slot_total):
@@ -57,6 +58,7 @@
         out_specs=pl.BlockSpec((column_total, groups, LANES), lambda g: (0, 0, 0)),
         out_shape=jax.ShapeDtypeStruct((column_total, groups, LANES), jnp.bfloat16),
         scratch_shapes=[pltpu.VMEM((column_total * groups, LANES), jnp.float32)],
+        compiler_params=PARAMS,
         name="transform",
     )(table, fields)
 
@@ -110,8 +112,10 @@
     steps_most = pl.cdiv(max(depths) - 1, STEPS) * STEPS + 1
     return pl.pallas_call(
         lambda *refs: basis_kernel(*refs, depths=depths, offsets=offsets),
-        out_shape=jax.ShapeDtypeStruct((sum(depths), lat_total), jnp.bfloat16),
+        out_shape=pltpu.VMEM((sum(depths), lat_total), jnp.bfloat16),
         scratch_shapes=[pltpu.VMEM((lat_total // LANES, steps_most * SUB, LANES), jnp.float32)],
+        out_specs=pl.BlockSpec(memory_space=pltpu.VMEM),
+        compiler_params=PARAMS,
         name="basis",
     )(order, cosine, start)
 
@@ -197,9 +201,15 @@
     shape = (spread, months // 4, LANES) if spread else (months, months)
     return pl.pallas_call(
         lambda *refs: gram_kernel(*refs, depths=depths, offsets=offsets, row_low=row_low),
-        out_shape=jax.ShapeDtypeStruct(shape, jnp.float32),
+        in_specs=[pl.BlockSpec(memory_space=pltpu.VMEM)] * 2,
+        out_specs=pl.BlockSpec(memory_space=pltpu.VMEM),
+        out_shape=pltpu.VMEM(shape, jnp.float32),
+        compiler_params=PARAMS,
         name="gram",
-    )(moved, basis)
+    )(
+        pltpu.with_memory_space_constraint(moved, pltpu.VMEM),
+        pltpu.with_memory_space_constraint(basis, pltpu.VMEM),
+    )
 
 
 def finish_kernel(parts_ref, out_ref):
@@ -265,7 +275,8 @@
         return pl.pallas_call(
             finish_kernel,
             out_shape=jax.ShapeDtypeStruct((month_count, months), jnp.float32),
-            name="finish",
+            compiler_params=PARAMS,
+        name="finish",
         )(parts)
     gram = lax.psum(gram, ("lat", "tm"))
     trace = jnp.sum(jnp.diagonal(gram))

time: 71 us -> 68.2 us (0.961)
  Pallas kernels: 19.1 us -> 12.6 us
  waiting for transfers between devices: 27.2 us -> 30.5 us
  local copies, waits for them, and re-layouts: 1.78 us -> 3.03 us
    all_to_all x1, waiting for transfers between devices: 27.2 us -> 30.5 us  [local(): lax.all_to_all(fourier, ('lat', 'tm'), split_axis=0, concat_axis=0, tiled...]
    pallas_call x1, Pallas kernels: 5.94 us -> 3.79 us  [basis_blocks(): pl.pallas_call(lambda *refs: basis_kernel(*refs, depths=depths, offsets=o...]
    pallas_call x1, Pallas kernels: 5.63 us -> 3.58 us  [longitude_transform(): pl.pallas_call(transform_kernel, grid=(row_count // rows_step,), in_specs...]
    unnamed x6 -> x10, local copies, waits for them, and re-layouts: 1.11 us -> 2.96 us
    pallas_call x1, Pallas kernels: 5.74 us -> 4.37 us  [gram_terms(): pl.pallas_call(lambda *refs: gram_kernel(*refs, depths=depths, offsets=of...]
    pallas_call x1, Pallas kernels: 1.78 us -> 0.83 us  [local(): pl.pallas_call(finish_kernel, out_shape=jax.ShapeDtypeStruct((month_count...]
  transfers between devices with their start and end apart: 1 -> 1, of which waited for: 1 -> 1; matrix products, arithmetic and copies ran while one was open for 2% -> 0% of each run, Pallas kernels for 8% -> 6%
where the time goes in v3:
time: 68.2 us; the launch traced here: 67.9 us
  waiting for transfers between devices  30.5 us (45%)
  blocking collectives  14.1 us (21%)
  Pallas kernels  12.6 us (18%)
  starting transfers between devices  7.44 us (11%)
  local copies, waits for them, and re-layouts  3.03 us (4%)
    all_to_all x1, waiting for transfers between devices, local(): lax.all_to_all(fourier, ('lat', 'tm'), split_axis=0, concat_axis=0, tiled...  30.5 us
    all_to_all x1, blocking collectives, local(): lax.all_to_all(gram, ('lat', 'tm'), split_axis=0, concat_axis=0, tiled=True)  14.1 us
    all_to_all x1, starting transfers between devices, local(): lax.all_to_all(fourier, ('lat', 'tm'), split_axis=0, concat_axis=0, tiled...  7.44 us
    pallas_call x1, Pallas kernels, gram_terms(): pl.pallas_call(lambda *refs: gram_kernel(*refs, depths=depths, offsets=of...  4.37 us
    pallas_call x1, Pallas kernels, basis_blocks(): pl.pallas_call(lambda *refs: basis_kernel(*refs, depths=depths, offsets=o...  3.79 us
    pallas_call x1, Pallas kernels, longitude_transform(): pl.pallas_call(transform_kernel, grid=(row_count // rows_step,), in_specs...  3.58 us
    unnamed x10, local copies, waits for them, and re-layouts  2.96 us
  transfers between devices with their start and end apart: 1, of which 1 were waited for; matrix products, arithmetic and copies ran while one was open for 0% of the time, Pallas kernels for 6%

profile of v3, /device:TPU:0, one launch (start us, length us, event | category | flops | bytes accessed | tf_op | source)
XLA Modules:
  0.0 67.9 jit_solution(7525883265164767006)
XLA Ops:
  0.0 0.0 copy-start
  0.0 1.6 %copy-done = bf16[32,32,1024]{2,1,0:T(8,128)(2,1)S(1)} copy-done((bf16[32,32,1024]{2,1,0:T(8,128)(2,1)S(1)}, bf16[32,32,1024]{2,1,0:T(8,128)(2,1)}, u32[]{:S(2)}) %copy-start) | copy-done | bytes 2097176
  1.6 0.0 copy-start.1
  1.6 1.4 %copy-done.1 = bf16[704,1024]{1,0:T(8,128)(2,1)S(1)} copy-done((bf16[704,1024]{1,0:T(8,128)(2,1)S(1)}, bf16[704,1024]{1,0:T(8,128)(2,1)}, u32[]{:S(2)}) %copy-start.1) | copy-done | bytes 1441816
  3.0 3.6 %transform.1 = bf16[704,8,128]{2,1,0:T(8,128)(2,1)} custom-call(bf16[704,1024]{1,0:T(8,128)(2,1)S(1)} %copy-done.1, bf16[32,32,1024]{2,1,0:T(8,128)(2,1)S(1)} %copy-done), custom_call_target="tpu_custom_call" | custom-call | tf_op jit(solution)/shard_map/transform/pallas_call | solution.py:51
  6.5 0.0 copy-start.3
  6.5 0.0 copy-start.4
  6.5 0.0 copy-start.2
  6.5 7.4 %all-to-all-start = ((bf16[32,22,8,128]{3,2,1,0:T(8,128)(2,1)}), bf16[32,22,8,128]{3,2,1,0:T(8,128)(2,1)}, u32[]{:S(2)}, u32[]{:S(2)}) async-start(bf16[32,22,8,128]{3,2,1,0:T(8,128)(2,1)} %bitcast), calls=%async_computation | async-start | bytes 2883584 | tf_op jit(solution)/shard_map/all_to_all | solution.py:247
  14.0 0.1 fusion
  14.1 0.0 copy-done.3
  14.1 0.0 copy-done.4
  14.1 0.1 multiply_multiply_fusion.refs_2_
  14.2 0.1 broadcast_in_dim.12.refs_0_
  14.3 0.0 copy-done.2
  14.3 3.8 %basis.1.refs_1_ = bf16[2112,512]{1,0:T(8,128)(2,1)S(1)} custom-call(f32[16,128]{1,0:T(8,128)S(1)} %broadcast_in_dim.12.refs_0_, f32[1,512]{1,0:T(1,128)S(1)} %copy-done.2, f32[16,512]{1,0:T(8,128)S(1)} %multiply_multiply_fusion.refs_2_), custom_call_target="tpu_custom_call" | custom-call | tf_op jit(solution)/shard_map/basis/pallas_call | solution.py:113
  18.1 30.5 %all-to-all-done = bf16[32,22,8,128]{3,2,1,0:T(8,128)(2,1)} async-done(((bf16[32,22,8,128]{3,2,1,0:T(8,128)(2,1)}), bf16[32,22,8,128]{3,2,1,0:T(8,128)(2,1)}, u32[]{:S(2)}, u32[]{:S(2)}) %all-to-all-start) | async-done | bytes 1441824 | tf_op jit(solution)/shard_map/all_to_all | solution.py:247
  48.6 4.4 %gram.1 = f32[32,16,128]{2,1,0:T(8,128)S(1)} custom-call(bf16[16,2,11,2,8,128]{5,4,3,2,1,0:T(8,128)(2,1)} %bitcast.1.refs_0_, bf16[2112,512]{1,0:T(8,128)(2,1)S(1)} %basis.1.refs_1_), custom_call_target="tpu_custom_call" | custom-call | tf_op jit(solution)/shard_map/gram/pallas_call | solution.py:202
  53.0 14.1 %all_to_all.10.parts_ref = f32[32,16,128]{2,1,0:T(8,128)S(1)} all-to-all(f32[32,16,128]{2,1,0:T(8,128)S(1)} %gram.1), channel_id=1, replica_groups=mesh['lat'=16,'tm'=2] {'lat','tm'}, dimensions={0} | all-to-all | bytes 524288 | tf_op jit(solution)/shard_map/all_to_all | solution.py:274
  67.1 0.8 %finish.1 = f32[32,64]{1,0:T(8,128)} custom-call(f32[32,16,128]{2,1,0:T(8,128)S(1)} %all_to_all.10.parts_ref), custom_call_target="tpu_custom_call" | custom-call | tf_op jit(solution)/shard_map/finish/pallas_call | solution.py:275
  (1 shorter events, 0.0 us)
Async XLA Ops:
  0.0 1.6 %copy-start = (bf16[32,32,1024]{2,1,0:T(8,128)(2,1)S(1)}, bf16[32,32,1024]{2,1,0:T(8,128)(2,1)}, u32[]{:S(2)}) copy-start(bf16[32,32,1024]{2,1,0:T(8,128)(2,1)} %fields_ref.1) | copy-start | bytes 6291460
  1.6 1.4 %copy-start.1 = (bf16[704,1024]{1,0:T(8,128)(2,1)S(1)}, bf16[704,1024]{1,0:T(8,128)(2,1)}, u32[]{:S(2)}) copy-start(bf16[704,1024]{1,0:T(8,128)(2,1)} %constant.102.clone.table_ref) | copy-start | bytes 4325380
  6.5 7.6 %copy-start.3 = (f32[512]{0:T(512)S(1)}, f32[512]{0:T(512)}, u32[]{:S(2)}) copy-start(f32[512]{0:T(512)} %constant.112) | copy-start | bytes 6148
  6.5 7.6 %copy-start.4 = (f32[512]{0:T(512)S(1)}, f32[512]{0:T(512)}, u32[]{:S(2)}) copy-start(f32[512]{0:T(512)} %constant.110) | copy-start | bytes 6148
  6.5 7.7 %copy-start.2 = (f32[1,512]{1,0:T(1,128)S(1)}, f32[1,512]{1,0:T(1,128)}, u32[]{:S(2)}) copy-start(f32[1,512]{1,0:T(1,128)} %constant.107.refs_1_) | copy-start | bytes 6148
  6.5 42.1 %all-to-all-start = ((bf16[32,22,8,128]{3,2,1,0:T(8,128)(2,1)}), bf16[32,22,8,128]{3,2,1,0:T(8,128)(2,1)}, u32[]{:S(2)}, u32[]{:S(2)}) async-start(bf16[32,22,8,128]{3,2,1,0:T(8,128)(2,1)} %bitcast), calls=%async_computation | async-start | bytes 2883584 | tf_op jit(solution)/shard_map/all_to_all | solution.py:247

commit v4 on v3

--- a/solution.py
+++ b/solution.py
@@ -60,7 +60,10 @@
         scratch_shapes=[pltpu.VMEM((column_total * groups, LANES), jnp.float32)],
         compiler_params=PARAMS,
         name="transform",
-    )(table, fields)
+    )(
+        pltpu.with_memory_space_constraint(table, pltpu.HBM),
+        pltpu.with_memory_space_constraint(fields, pltpu.HBM),
+    )
 
 
 def basis_kernel(order_ref, cosine_ref, start_ref, out_ref, scratch_ref, *, depths, offsets):

time: 68.2 us -> 67.3 us (0.987)
  local copies, waits for them, and re-layouts: 3.03 us -> 0.08 us
  Pallas kernels: 12.6 us -> 14.6 us
    unnamed x10 -> x6, local copies, waits for them, and re-layouts: 2.96 us -> 0.01 us
    pallas_call x1, Pallas kernels: 3.58 us -> 5.62 us  [longitude_transform(): pl.pallas_call(transform_kernel, grid=(row_count // rows_step,), in_specs...]
where the time goes in v4:
time: 67.3 us; the launch traced here: 67 us
  waiting for transfers between devices  30.5 us (45%)
  Pallas kernels  14.6 us (22%)
  blocking collectives  14.1 us (21%)
  starting transfers between devices  7.43 us (11%)
    all_to_all x1, waiting for transfers between devices, local(): lax.all_to_all(fourier, ('lat', 'tm'), split_axis=0, concat_axis=0, tiled...  30.5 us
    all_to_all x1, blocking collectives, local(): lax.all_to_all(gram, ('lat', 'tm'), split_axis=0, concat_axis=0, tiled=True)  14.1 us
    all_to_all x1, starting transfers between devices, local(): lax.all_to_all(fourier, ('lat', 'tm'), split_axis=0, concat_axis=0, tiled...  7.43 us
    pallas_call x1, Pallas kernels, longitude_transform(): pl.pallas_call(transform_kernel, grid=(row_count // rows_step,), in_specs...  5.62 us
    pallas_call x1, Pallas kernels, gram_terms(): pl.pallas_call(lambda *refs: gram_kernel(*refs, depths=depths, offsets=of...  4.37 us
    pallas_call x1, Pallas kernels, basis_blocks(): pl.pallas_call(lambda *refs: basis_kernel(*refs, depths=depths, offsets=o...  3.79 us
  transfers between devices with their start and end apart: 1, of which 1 were waited for; matrix products, arithmetic and copies ran while one was open for 0% of the time, Pallas kernels for 6%

profile of v4, /device:TPU:0, one launch (start us, length us, event | category | flops | bytes accessed | tf_op | source)
XLA Modules:
  0.0 67.0 jit_solution(13033241995470076288)
XLA Ops:
  0.0 5.6 %transform.1 = bf16[704,8,128]{2,1,0:T(8,128)(2,1)} custom-call(bf16[704,1024]{1,0:T(8,128)(2,1)} %constant.102.clone.table_ref, bf16[32,32,1024]{2,1,0:T(8,128)(2,1)} %fields_ref.1), custom_call_target="tpu_custom_call" | custom-call | tf_op jit(solution)/shard_map/transform/pallas_call | solution.py:51
  5.6 0.0 copy-start.1
  5.6 0.0 copy-start.2
  5.6 0.0 copy-start
  5.6 7.4 %all-to-all-start = ((bf16[32,22,8,128]{3,2,1,0:T(8,128)(2,1)}), bf16[32,22,8,128]{3,2,1,0:T(8,128)(2,1)}, u32[]{:S(2)}, u32[]{:S(2)}) async-start(bf16[32,22,8,128]{3,2,1,0:T(8,128)(2,1)} %bitcast), calls=%async_computation | async-start | bytes 2883584 | tf_op jit(solution)/shard_map/all_to_all | solution.py:250
  13.1 0.1 fusion
  13.2 0.0 copy-done.1
  13.2 0.0 copy-done.2
  13.2 0.1 multiply_multiply_fusion.refs_2_
  13.3 0.1 broadcast_in_dim.12.refs_0_
  13.3 0.0 copy-done
  13.3 3.8 %basis.1.refs_1_ = bf16[2112,512]{1,0:T(8,128)(2,1)S(1)} custom-call(f32[16,128]{1,0:T(8,128)S(1)} %broadcast_in_dim.12.refs_0_, f32[1,512]{1,0:T(1,128)S(1)} %copy-done, f32[16,512]{1,0:T(8,128)S(1)} %multiply_multiply_fusion.refs_2_), custom_call_target="tpu_custom_call" | custom-call | tf_op jit(solution)/shard_map/basis/pallas_call | solution.py:116
  17.1 30.5 %all-to-all-done = bf16[32,22,8,128]{3,2,1,0:T(8,128)(2,1)} async-done(((bf16[32,22,8,128]{3,2,1,0:T(8,128)(2,1)}), bf16[32,22,8,128]{3,2,1,0:T(8,128)(2,1)}, u32[]{:S(2)}, u32[]{:S(2)}) %all-to-all-start) | async-done | bytes 1441824 | tf_op jit(solution)/shard_map/all_to_all | solution.py:250
  47.7 4.4 %gram.1 = f32[32,16,128]{2,1,0:T(8,128)S(1)} custom-call(bf16[16,2,11,2,8,128]{5,4,3,2,1,0:T(8,128)(2,1)} %bitcast.1.refs_0_, bf16[2112,512]{1,0:T(8,128)(2,1)S(1)} %basis.1.refs_1_), custom_call_target="tpu_custom_call" | custom-call | tf_op jit(solution)/shard_map/gram/pallas_call | solution.py:205
  52.1 14.1 %all_to_all.10.parts_ref = f32[32,16,128]{2,1,0:T(8,128)S(1)} all-to-all(f32[32,16,128]{2,1,0:T(8,128)S(1)} %gram.1), channel_id=1, replica_groups=mesh['lat'=16,'tm'=2] {'lat','tm'}, dimensions={0} | all-to-all | bytes 524288 | tf_op jit(solution)/shard_map/all_to_all | solution.py:277
  66.2 0.8 %finish.1 = f32[32,64]{1,0:T(8,128)} custom-call(f32[32,16,128]{2,1,0:T(8,128)S(1)} %all_to_all.10.parts_ref), custom_call_target="tpu_custom_call" | custom-call | tf_op jit(solution)/shard_map/finish/pallas_call | solution.py:278
  (1 shorter events, 0.0 us)
Async XLA Ops:
  5.6 7.5 %copy-start.1 = (f32[512]{0:T(512)S(1)}, f32[512]{0:T(512)}, u32[]{:S(2)}) copy-start(f32[512]{0:T(512)} %constant.112) | copy-start | bytes 6148
  5.6 7.5 %copy-start.2 = (f32[512]{0:T(512)S(1)}, f32[512]{0:T(512)}, u32[]{:S(2)}) copy-start(f32[512]{0:T(512)} %constant.110) | copy-start | bytes 6148
  5.6 7.7 %copy-start = (f32[1,512]{1,0:T(1,128)S(1)}, f32[1,512]{1,0:T(1,128)}, u32[]{:S(2)}) copy-start(f32[1,512]{1,0:T(1,128)} %constant.107.refs_1_) | copy-start | bytes 6148
  5.6 42.1 %all-to-all-start = ((bf16[32,22,8,128]{3,2,1,0:T(8,128)(2,1)}), bf16[32,22,8,128]{3,2,1,0:T(8,128)(2,1)}, u32[]{:S(2)}, u32[]{:S(2)}) async-start(bf16[32,22,8,128]{3,2,1,0:T(8,128)(2,1)} %bitcast), calls=%async_computation | async-start | bytes 2883584 | tf_op jit(solution)/shard_map/all_to_all | solution.py:250

commit v5 on v4

--- a/solution.py
+++ b/solution.py
@@ -144,12 +144,13 @@
     return pieces
 
 
-def gram_kernel(moved_ref, basis_ref, out_ref, *, depths, offsets, row_low):
-    lat_devices, tm_devices, _, _, groups, _ = moved_ref.shape
+def gram_kernel(early_ref, late_ref, basis_ref, out_ref, *, depths, offsets, row_low):
+    lat_devices, tm_devices, early, _, groups, _ = early_ref.shape
     total = None
     for slot, depth in enumerate(depths):
+        moved_ref, place = (early_ref, slot) if slot < early else (late_ref, slot - early)
         pieces = [
-            moved_ref[:, tm, slot, part].astype(jnp.float32).reshape(lat_devices * groups, LANES)
+            moved_ref[:, tm, place, part].astype(jnp.float32).reshape(lat_devices * groups, LANES)
             for part in range(2)
             for tm in range(tm_devices)
         ]
@@ -200,17 +201,17 @@
 
 
 def gram_terms(moved, basis, depths, offsets, row_low, spread):
-    months = moved.shape[1] * (LANES // row_low)
+    months = moved[0].shape[1] * (LANES // row_low)
     shape = (spread, months // 4, LANES) if spread else (months, months)
     return pl.pallas_call(
         lambda *refs: gram_kernel(*refs, depths=depths, offsets=offsets, row_low=row_low),
-        in_specs=[pl.BlockSpec(memory_space=pltpu.VMEM)] * 2,
+        in_specs=[pl.BlockSpec(memory_space=pltpu.VMEM)] * 3,
         out_specs=pl.BlockSpec(memory_space=pltpu.VMEM),
         out_shape=pltpu.VMEM(shape, jnp.float32),
         compiler_params=PARAMS,
         name="gram",
     )(
-        pltpu.with_memory_space_constraint(moved, pltpu.VMEM),
+        *(pltpu.with_memory_space_constraint(part, pltpu.VMEM) for part in moved),
         pltpu.with_memory_space_constraint(basis, pltpu.VMEM),
     )
 
@@ -244,11 +245,16 @@
     depths = [-(-(TRUNC + 1 - slot * device_total) // 16) * 16 for slot in range(slots)]
     offsets = [sum(depths[:slot]) for slot in range(slots)]
 
-    table = jnp.asarray(transform_table(lon_count, device_total, slots))
-    fourier = longitude_transform(fields, table, groups)
-    fourier = fourier.reshape(device_total, slots * 2, groups, LANES)
-    moved = lax.all_to_all(fourier, ("lat", "tm"), split_axis=0, concat_axis=0, tiled=True)
-    moved = moved.reshape(lat_devices, tm_devices, slots, 2, groups, LANES)
+    table = transform_table(lon_count, device_total, slots)
+    table = table.reshape(device_total, slots * 2, lon_count)
+    moved = []
+    split = slots // 2
+    for begin, end in ((0, split), (split, slots)) if split else ((0, slots), (0, slots)):
+        part = jnp.asarray(table[:, 2 * begin : 2 * end].reshape(-1, lon_count))
+        fourier = longitude_transform(fields, part, groups)
+        fourier = fourier.reshape(device_total, (end - begin) * 2, groups, LANES)
+        part = lax.all_to_all(fourier, ("lat", "tm"), split_axis=0, concat_axis=0, tiled=True)
+        moved.append(part.reshape(lat_devices, tm_devices, end - begin, 2, groups, LANES))
 
     latitude = np.arange(lat_count).reshape(lat_devices, groups, row_low)
     latitude = jnp.asarray(latitude.transpose(2, 0, 1).reshape(1, -1))

time: 67.3 us -> 73.2 us (1.088)
  starting transfers between devices: 7.43 us -> 11 us
  Pallas kernels: 14.6 us -> 16.6 us
  local copies, waits for them, and re-layouts: 0.08 us -> 1.18 us
  waiting for transfers between devices: 30.5 us -> 29.6 us
    all_to_all x1 -> x2, starting transfers between devices: 7.43 us -> 11 us  [local(): lax.all_to_all(fourier, ('lat', 'tm'), split_axis=0, concat_axis=0, tiled...]
    pallas_call x1 -> x2, Pallas kernels: 5.62 us -> 8.98 us  [longitude_transform(): pl.pallas_call(transform_kernel, grid=(row_count // rows_step,), in_specs...]
    pallas_call x1, Pallas kernels: 4.37 us -> 3.01 us  [gram_terms(): pl.pallas_call(lambda *refs: gram_kernel(*refs, depths=depths, offsets=of...]
    unnamed x6 -> x10, local copies, waits for them, and re-layouts: 0.01 us -> 1.11 us
    all_to_all x1 -> x2, waiting for transfers between devices: 30.5 us -> 29.6 us  [local(): lax.all_to_all(fourier, ('lat', 'tm'), split_axis=0, concat_axis=0, tiled...]
  transfers between devices with their start and end apart: 1 -> 2, of which waited for: 1 -> 2; matrix products, arithmetic and copies ran while one was open for 0% -> 0% of each run, Pallas kernels for 6% -> 12%
where the time goes in v5:
time: 73.2 us; the launch traced here: 72.8 us
  waiting for transfers between devices  29.6 us (40%)
  Pallas kernels  16.6 us (23%)
  blocking collectives  14.1 us (19%)
  starting transfers between devices  11 us (15%)
  local copies, waits for them, and re-layouts  1.18 us (2%)
    all_to_all x2, waiting for transfers between devices, local(): lax.all_to_all(fourier, ('lat', 'tm'), split_axis=0, concat_axis=0, tiled...  29.6 us
    all_to_all x1, blocking collectives, local(): lax.all_to_all(gram, ('lat', 'tm'), split_axis=0, concat_axis=0, tiled=True)  14.1 us
    all_to_all x2, starting transfers between devices, local(): lax.all_to_all(fourier, ('lat', 'tm'), split_axis=0, concat_axis=0, tiled...  11 us
    pallas_call x2, Pallas kernels, longitude_transform(): pl.pallas_call(transform_kernel, grid=(row_count // rows_step,), in_specs...  8.98 us
    pallas_call x1, Pallas kernels, basis_blocks(): pl.pallas_call(lambda *refs: basis_kernel(*refs, depths=depths, offsets=o...  3.79 us
    pallas_call x1, Pallas kernels, gram_terms(): pl.pallas_call(lambda *refs: gram_kernel(*refs, depths=depths, offsets=of...  3.01 us
  transfers between devices with their start and end apart: 2, of which 2 were waited for; matrix products, arithmetic and copies ran while one was open for 0% of the time, Pallas kernels for 12%

profile of v5, /device:TPU:0, one launch (start us, length us, event | category | flops | bytes accessed | tf_op | source)
XLA Modules:
  0.0 72.8 jit_solution(16145850473511818408)
XLA Ops:
  0.0 4.4 %transform.2 = bf16[320,8,128]{2,1,0:T(8,128)(2,1)} custom-call(bf16[320,1024]{1,0:T(8,128)(2,1)} %constant.104.clone.table_ref, bf16[32,32,1024]{2,1,0:T(8,128)(2,1)} %fields_ref.3), custom_call_target="tpu_custom_call" | custom-call | tf_op jit(solution)/shard_map/transform/pallas_call | solution.py:51
  4.4 7.3 %all-to-all-start = ((bf16[32,10,8,128]{3,2,1,0:T(8,128)(2,1)}), bf16[32,10,8,128]{3,2,1,0:T(8,128)(2,1)S(1)}, u32[]{:S(2)}, u32[]{:S(2)}) async-start(bf16[32,10,8,128]{3,2,1,0:T(8,128)(2,1)} %bitcast), calls=%async_computation | async-start | bytes 1310720 | tf_op jit(solution)/shard_map/all_to_all | solution.py:256
  11.7 0.0 copy-start.3
  11.7 0.0 copy-start.4
  11.8 0.0 copy-start.2
  11.8 4.6 %transform.3 = bf16[384,8,128]{2,1,0:T(8,128)(2,1)} custom-call(bf16[384,1024]{1,0:T(8,128)(2,1)} %constant.105.clone.table_ref, bf16[32,32,1024]{2,1,0:T(8,128)(2,1)} %fields_ref.3), custom_call_target="tpu_custom_call" | custom-call | tf_op jit(solution)/shard_map/transform/pallas_call | solution.py:51
  16.4 13.1 %all-to-all-done = bf16[32,10,8,128]{3,2,1,0:T(8,128)(2,1)S(1)} async-done(((bf16[32,10,8,128]{3,2,1,0:T(8,128)(2,1)}), bf16[32,10,8,128]{3,2,1,0:T(8,128)(2,1)S(1)}, u32[]{:S(2)}, u32[]{:S(2)}) %all-to-all-start) | async-done | bytes 655392 | tf_op jit(solution)/shard_map/all_to_all | solution.py:256
  29.5 0.0 copy-start
  29.5 3.6 %all-to-all-start.1 = ((bf16[32,12,8,128]{3,2,1,0:T(8,128)(2,1)}), bf16[32,12,8,128]{3,2,1,0:T(8,128)(2,1)S(1)}, u32[]{:S(2)}, u32[]{:S(2)}) async-start(bf16[32,12,8,128]{3,2,1,0:T(8,128)(2,1)} %bitcast.2), calls=%async_computation.1 | async-start | bytes 1572864 | tf_op jit(solution)/shard_map/all_to_all | solution.py:256
  33.2 0.1 fusion
  33.2 0.0 copy-done.3
  33.2 0.0 copy-done.4
  33.3 0.1 multiply_multiply_fusion.refs_2_
  33.3 0.0 copy-done
  33.4 0.1 broadcast_in_dim.12.refs_0_
  33.4 0.0 copy-done.2
  33.4 3.8 %basis.1.refs_2_ = bf16[2112,512]{1,0:T(8,128)(2,1)S(1)} custom-call(f32[16,128]{1,0:T(8,128)S(1)} %broadcast_in_dim.12.refs_0_, f32[1,512]{1,0:T(1,128)S(1)} %copy-done.2, f32[16,512]{1,0:T(8,128)S(1)} %multiply_multiply_fusion.refs_2_), custom_call_target="tpu_custom_call" | custom-call | tf_op jit(solution)/shard_map/basis/pallas_call | solution.py:116
  37.2 16.5 %all-to-all-done.1 = bf16[32,12,8,128]{3,2,1,0:T(8,128)(2,1)S(1)} async-done(((bf16[32,12,8,128]{3,2,1,0:T(8,128)(2,1)}), bf16[32,12,8,128]{3,2,1,0:T(8,128)(2,1)S(1)}, u32[]{:S(2)}, u32[]{:S(2)}) %all-to-all-start.1) | async-done | bytes 786464 | tf_op jit(solution)/shard_map/all_to_all | solution.py:256
  53.7 0.0 copy-start.1
  53.7 1.1 %copy-done.1 = bf16[32,10,8,128]{3,2,1,0:T(8,128)(2,1)S(1)} copy-done((bf16[32,10,8,128]{3,2,1,0:T(8,128)(2,1)S(1)}, bf16[32,10,8,128]{3,2,1,0:T(8,128)(2,1)}, u32[]{:S(2)}) %copy-start.1) | copy-done | bytes 655384
  54.8 3.0 %gram.1 = f32[32,16,128]{2,1,0:T(8,128)S(1)} custom-call(bf16[16,2,5,2,8,128]{5,4,3,2,1,0:T(8,128)(2,1)S(1)} %bitcast.5, bf16[16,2,6,2,8,128]{5,4,3,2,1,0:T(8,128)(2,1)S(1)} %bitcast.4, bf16[2112,512]{1,0:T(8,128)(2,1)S(1)} %basis.1.refs_2_), custom_call_target="tpu_custom_call" | custom-call | tf_op jit(solution)/shard_map/gram/pallas_call | solution.py:206
  57.8 14.1 %all_to_all.15.parts_ref = f32[32,16,128]{2,1,0:T(8,128)S(1)} all-to-all(f32[32,16,128]{2,1,0:T(8,128)S(1)} %gram.1), channel_id=1, replica_groups=mesh['lat'=16,'tm'=2] {'lat','tm'}, dimensions={0} | all-to-all | bytes 524288 | tf_op jit(solution)/shard_map/all_to_all | solution.py:283
  71.9 0.8 %finish.1 = f32[32,64]{1,0:T(8,128)} custom-call(f32[32,16,128]{2,1,0:T(8,128)S(1)} %all_to_all.15.parts_ref), custom_call_target="tpu_custom_call" | custom-call | tf_op jit(solution)/shard_map/finish/pallas_call | solution.py:284
  (1 shorter events, 0.0 us)
Async XLA Ops:
  4.4 25.1 %all-to-all-start = ((bf16[32,10,8,128]{3,2,1,0:T(8,128)(2,1)}), bf16[32,10,8,128]{3,2,1,0:T(8,128)(2,1)S(1)}, u32[]{:S(2)}, u32[]{:S(2)}) async-start(bf16[32,10,8,128]{3,2,1,0:T(8,128)(2,1)} %bitcast), calls=%async_computation | async-start | bytes 1310720 | tf_op jit(solution)/shard_map/all_to_all | solution.py:256
  11.7 21.5 %copy-start.3 = (f32[512]{0:T(512)S(1)}, f32[512]{0:T(512)}, u32[]{:S(2)}) copy-start(f32[512]{0:T(512)} %constant.115) | copy-start | bytes 6148
  11.7 21.5 %copy-start.4 = (f32[512]{0:T(512)S(1)}, f32[512]{0:T(512)}, u32[]{:S(2)}) copy-start(f32[512]{0:T(512)} %constant.113) | copy-start | bytes 6148
  11.8 21.7 %copy-start.2 = (f32[1,512]{1,0:T(1,128)S(1)}, f32[1,512]{1,0:T(1,128)}, u32[]{:S(2)}) copy-start(f32[1,512]{1,0:T(1,128)} %constant.110.refs_1_) | copy-start | bytes 6148
  29.5 3.8 %copy-start = (bf16[32,10,8,128]{3,2,1,0:T(8,128)(2,1)}, bf16[32,10,8,128]{3,2,1,0:T(8,128)(2,1)S(1)}, u32[]{:S(2)}) copy-start(bf16[32,10,8,128]{3,2,1,0:T(8,128)(2,1)S(1)} %all-to-all-done) | copy-start | bytes 1966084
  29.5 24.2 %all-to-all-start.1 = ((bf16[32,12,8,128]{3,2,1,0:T(8,128)(2,1)}), bf16[32,12,8,128]{3,2,1,0:T(8,128)(2,1)S(1)}, u32[]{:S(2)}, u32[]{:S(2)}) async-start(bf16[32,12,8,128]{3,2,1,0:T(8,128)(2,1)} %bitcast.2), calls=%async_computation.1 | async-start | bytes 1572864 | tf_op jit(solution)/shard_map/all_to_all | solution.py:256
  53.7 1.1 %copy-start.1 = (bf16[32,10,8,128]{3,2,1,0:T(8,128)(2,1)S(1)}, bf16[32,10,8,128]{3,2,1,0:T(8,128)(2,1)}, u32[]{:S(2)}) copy-start(bf16[32,10,8,128]{3,2,1,0:T(8,128)(2,1)} %copy-done) | copy-start | bytes 1966084
